TPU v7x, 32 devices: a whole 2x2x4 slice. The times are simulated.
32 devices in a mesh: grp: 4 (over y, x), clu: 8 (over z, core).
Axes of the slice: x: 2, y: 2, z: 4, core: 2. Of those that a mesh axis runs over, the one named last changes fastest.
Arguments:
- forces: bfloat16 [3, 2048, 512], P(None, 'clu'), may hold values from -6 to 6
- order: int32 [2048], P('clu'), may hold values from 0 to 2047, as said below
- bases: bfloat16 [2, 32, 3, 2048], P(None, None, None, 'clu'), may hold values from -0.21875 to 0.21875
- near_tiles: bfloat16 [8, 8, 768, 768], P('clu', 'grp'), may hold values from -0.078125 to 0.078125
- near_col: int32 [8, 8], P('clu', 'grp'), may hold values from 0 to 7, as said below
- far_basis: bfloat16 [8, 64, 32, 768], P('clu', 'grp'), may hold values from -0.125 to 0.125
- far_coupling: bfloat16 [8, 64, 32, 32], P('clu', 'grp'), may hold values from -1 to 1
- far_scale: float32 [8, 64], P('clu', 'grp'), may hold values from 0.5 to 2
- far_rank: int32 [8, 64], P('clu', 'grp'), may hold values from 8 to 32
- far_target: int32 [8, 64], P('clu', 'grp'), may hold values from 0 to 5, as said below
Outputs:
- velocity: float32 [3, 2048, 512], P(None, 'clu', 'grp')
Inputs may be any that keep to these rules, and one draw needn't show every extreme that they name: `order`: A permutation of the bead numbers; the 256 positions of row block c hold beads of chain blocks c - 1, c and c + 1 only, counted cyclically, exactly 64 of them from chain block c - 1 and exactly 64 from chain block c + 1. `near_col`: each near tile's column block lies within two blocks of its row block, counted cyclically. `far_target`: level l takes indices 2 ** (l + 1) - 2 to 2 ** (l + 2) - 3; the named cluster never contains the block's own row block.
All inputs are finite; a program needn't handle non-finite values.
Results may differ from a plain program's by a relative error of at most 0.0025.
Values may be sent and summed in bfloat16 or wider, within the bound.
A program may use at most 64 MiB of HBM per device.

v0:
```python
import jax
import jax.numpy as jnp
from jax import lax
from jax.sharding import PartitionSpec as P


def with_halo(cells, sides, width):
    for axis, dim in sides:
        count = lax.axis_size(axis)
        head = lax.slice_in_dim(cells, 0, width, axis=dim)
        tail = lax.slice_in_dim(cells, cells.shape[dim] - width, cells.shape[dim], axis=dim)
        cells = jnp.concatenate(
            [
                lax.ppermute(tail, axis, [(i, (i + 1) % count) for i in range(count)]),
                cells,
                lax.ppermute(head, axis, [((i + 1) % count, i) for i in range(count)]),
            ],
            axis=dim,
        )
    return cells


def from_behind(shard, axis, by):
    size = lax.axis_size(axis)
    return lax.ppermute(shard, axis, [(i, (i + by) % size) for i in range(size)])


def slot_numbers(positions_order, source_block, tile_len):
    chosen = (positions_order // tile_len == source_block).astype(jnp.int32)
    ranked = jnp.cumsum(chosen) - 1
    return (chosen, ranked)


def rows_for(positions_order, source_block, tile_len, quarter):
    chosen, ranked = slot_numbers(positions_order, source_block, tile_len)
    slot_ids = jnp.arange(quarter, dtype=jnp.int32)
    onehot = (ranked[None, :] == slot_ids[:, None]).astype(jnp.int32) * chosen[None, :]
    local_rows = jnp.sum(onehot * (positions_order - source_block * tile_len)[None, :], axis=1)
    return local_rows


def nearby_forces(local_forces, order, clusters, own_index):
    tile_len = order.shape[0]
    quarter = tile_len // 4
    rims = with_halo(order, (("clu", 0),), tile_len)
    order_prev = rims[:tile_len]
    order_next = rims[2 * tile_len :]
    send_next = jnp.take(local_forces, rows_for(order_next, own_index, tile_len, quarter), axis=1)
    send_prev = jnp.take(local_forces, rows_for(order_prev, own_index, tile_len, quarter), axis=1)
    from_prev = from_behind(send_next, "clu", 1)
    from_next = from_behind(send_prev, "clu", -1)
    stacked = jnp.concatenate([local_forces, from_prev, from_next], axis=1)
    prev_block = jnp.mod(own_index - 1, clusters)
    next_block = jnp.mod(own_index + 1, clusters)
    prev_mask, prev_rank = slot_numbers(order, prev_block, tile_len)
    next_mask, next_rank = slot_numbers(order, next_block, tile_len)
    own_rows = order - own_index * tile_len
    positions = jnp.where(
        prev_mask == 1,
        tile_len + prev_rank,
        jnp.where(next_mask == 1, tile_len + quarter + next_rank, own_rows),
    )
    own_block = jnp.take(stacked, positions, axis=1)
    pieces = {0: own_block}
    for offset in (-2, -1, 1, 2):
        pieces[offset] = from_behind(own_block, "clu", -offset)
    return jnp.concatenate([pieces[offset] for offset in (-2, -1, 0, 1, 2)], axis=1)


def on_device(
    forces,
    order,
    bases,
    near_tiles,
    near_col,
    far_basis,
    far_coupling,
    far_scale,
    far_rank,
    far_target,
):
    clusters = lax.axis_size("clu")
    own_index = lax.axis_index("clu")
    tile_len = order.shape[0]
    columns = forces.shape[2]
    nearby = nearby_forces(forces, order, clusters, own_index)
    own_forces = nearby[:, 2 * tile_len : 3 * tile_len, :].reshape(3 * tile_len, columns)
    tiles = near_tiles[0]
    positions = jnp.mod(near_col[0] - own_index + 2, clusters)
    partial_value = jnp.zeros((3 * tile_len, columns), jnp.float32)
    for slot in range(tiles.shape[0]):
        column_block = lax.dynamic_slice_in_dim(
            nearby, positions[slot] * tile_len, tile_len, 1
        ).reshape(3 * tile_len, columns)
        partial_value = partial_value + jnp.dot(
            tiles[slot], column_block, preferred_element_type=jnp.float32
        )
    levels = bases.shape[0]
    rank = bases.shape[1]
    flat_bases = bases.reshape(levels * rank, 3 * tile_len)
    pieces = jnp.dot(flat_bases, own_forces, preferred_element_type=jnp.float32).reshape(
        levels, rank, columns
    )
    coarse_count = 2 ** (levels + 1) - 2
    slots = jnp.arange(coarse_count, dtype=jnp.int32)
    table = jnp.zeros((coarse_count, rank, columns), jnp.float32)
    for level in range(levels):
        count = 2 ** (level + 1)
        members = clusters // count
        target_slot = count - 2 + own_index // members
        table = table + (slots == target_slot).astype(jnp.float32)[:, None, None] * pieces[level]
    table = lax.psum(table, "clu")
    targets = far_target[0]
    far_count = targets.shape[0]
    selector = (targets[:, None] == slots[None, :]).astype(jnp.float32)
    picked = jnp.dot(
        selector, table.reshape(coarse_count, rank * columns), precision=lax.Precision.HIGHEST
    ).reshape(far_count, rank, columns)
    keeping = (jnp.arange(rank, dtype=jnp.int32)[None, :] < far_rank[0][:, None]).astype(
        jnp.float32
    )
    masked = picked * keeping[:, :, None]
    coupled = jnp.einsum(
        "brs,bsn->brn", far_coupling[0].astype(jnp.float32), masked, precision=lax.Precision.HIGHEST
    )
    coupled = (coupled * far_scale[0][:, None, None]).astype(jnp.bfloat16)
    far_part = lax.dot_general(
        far_basis[0].reshape(far_count * rank, 3 * tile_len),
        coupled.reshape(far_count * rank, columns),
        (((0,), (0,)), ((), ())),
        preferred_element_type=jnp.float32,
    )
    partial_value = (partial_value + far_part).reshape(3, tile_len, columns)
    return lax.psum_scatter(partial_value, "grp", scatter_dimension=2, tiled=True)


def solution(mesh):
    placed = (
        P(None, "clu", None),
        P("clu"),
        P(None, None, None, "clu"),
        P("clu", "grp", None, None),
        P("clu", "grp"),
        P("clu", "grp", None, None),
        P("clu", "grp", None, None),
        P("clu", "grp"),
        P("clu", "grp"),
        P("clu", "grp"),
    )
    return jax.shard_map(
        on_device, mesh=mesh, in_specs=placed, out_specs=P(None, "clu", "grp"), check_vma=False
    )
```

profile of v0, /device:TPU:9, one launch (start us, length us, event | category | flops | bytes accessed | tf_op | source)
XLA Modules:
  0.0 158.7 jit_solution(16140917400354078159)
XLA Ops:
  6.6 0.7 collective-permute-start
  7.3 1.2 collective-permute-start.2
  8.6 0.7 and_select_fusion
  9.2 0.6 fusion.17
  11.0 1.8 %copy.43 = bf16[3,256,512]{2,0,1:T(4,128)(2,1)S(1)} copy(bf16[3,256,512]{2,1,0:T(8,128)(2,1)} %param.12) | data formatting | bytes 1572864 | tf_op args[0]
  15.7 1.2 gather_fusion.1
  17.0 0.5 collective-permute-start.1
  17.5 1.2 gather_fusion.2
  18.9 1.2 collective-permute-done.1
  20.3 5.8 %collective-permute-done.3 = bf16[3,64,512]{2,1,0:T(8,128)(2,1)S(1)} collective-permute-done((bf16[3,64,512]{2,1,0:T(8,128)(2,1)S(1)}, bf16[3,64,512]{2,1,0:T(8,128)(2,1)S(1)}, u32[]{:S(2)}, u32[]{:S(2)}) %collective-permute-start.3) | collective-permute-done | bytes 196640 | tf_op jit(solution)/shard_map/ppermute | solution.py:25
  26.2 2.1 %pad_maximum_fusion = bf16[3,384,512]{2,0,1:T(4,128)(2,1)} fusion(bf16[3,64,512]{2,0,1:T(4,128)(2,1)S(1)} %copy.45, bf16[3,64,512]{2,0,1:T(4,128)(2,1)S(1)} %copy.44, bf16[3,256,512]{2,0,1:T(4,128)(2,1)S(1)} %copy.43), kind=kLoop, calls=%fused_computation.3 | loop fusion | flops 1179648 | bytes 2359296 | tf_op jit(solution)/shard_map/concatenate | solution.py:52
  28.3 2.9 %gather_fusion = bf16[256,3,512]{2,1,0:T(4,128)(2,1)S(1)} fusion(bf16[3,384,512]{2,0,1:T(4,128)(2,1)} %pad_maximum_fusion, s32[1024]{0:T(1024)S(1)} %pad_clamp_fusion), kind=kCustom, calls=%fused_computation.2 | custom fusion | bytes 1573888 | tf_op jit(solution)/shard_map/jit(_take)/gather | solution.py:63
  31.3 1.0 select_bitcast_fusion
  32.5 0.5 collective-permute-start.4
  33.4 1.1 copy.69
  34.5 0.7 fusion.9
  35.7 1.0 collective-permute-start.7
  36.8 66.9 %all-reduce.2.cloned.1.call-done = f32[32,512,6]{1,2,0:T(8,128)} async-done(((f32[32,512,6]{1,2,0:T(8,128)}), f32[32,512,6]{1,2,0:T(8,128)}) %all-reduce.2.cloned.1.call-update) | async-done | bytes 393232 | tf_op jit(solution)/shard_map/psum | solution.py:112
  103.6 1.8 %convolution_multiply_fusion.1 = f32[16,32,512]{2,0,1:T(8,128)S(1)} fusion(f32[32,512,6]{1,2,0:T(8,128)} %all-reduce.2.cloned.1.call-done, f32[16,32]{0,1:T(8,128)S(1)} %fusion.9, s32[16]{0:T(128)} %bitcast.86), kind=kOutput, calls=%fused_computation.6 | convolution fusion | flops 19136608 | bytes 1443904 | tf_op jit(solution)/shard_map/dot_general | solution.py:116
  105.4 1.3 fusion
  106.7 0.7 copy_dynamic-update-slice_fusion.3
  107.4 1.9 %copy_dynamic-update-slice_fusion.2 = bf16[3,1280,512]{2,0,1:T(4,128)(2,1)S(1)} fusion(bf16[3,1280,512]{2,0,1:T(4,128)(2,1)S(1)} %copy_dynamic-update-slice_fusion.3, bf16[3,256,512]{2,1,0:T(8,128)(2,1)} %collective-permute-done.5), kind=kLoop, calls=%fused_computation.18 | loop fusion | bytes 1835008
  109.3 1.2 constant_dynamic-update-slice_fusion
  110.5 1.9 %copy_dynamic-update-slice_fusion.1 = bf16[3,1280,512]{2,0,1:T(4,128)(2,1)S(1)} fusion(bf16[3,1280,512]{2,0,1:T(4,128)(2,1)S(1)} %constant_dynamic-update-slice_fusion, bf16[3,256,512]{2,1,0:T(8,128)(2,1)} %collective-permute-done.6), kind=kLoop, calls=%fused_computation.17 | loop fusion | bytes 1835008
  112.4 1.9 %copy_dynamic-update-slice_fusion = bf16[3,1280,512]{2,0,1:T(4,128)(2,1)S(1)} fusion(bf16[3,1280,512]{2,0,1:T(4,128)(2,1)S(1)} %copy_dynamic-update-slice_fusion.1, bf16[3,256,512]{2,1,0:T(8,128)(2,1)} %collective-permute-done.7), kind=kLoop, calls=%fused_computation.16 | loop fusion | bytes 1835008 | tf_op jit(solution)/shard_map/concatenate | solution.py:67
  114.3 0.7 constant_dynamic-slice_fusion
  115.4 1.3 copy-done.8
  116.7 0.8 fusion.1
  117.5 0.8 fusion.3
  118.4 0.6 add_bitcast_fusion
  119.0 1.6 %copy.59 = f32[768,512]{1,0:T(8,128)} copy(f32[768,512]{0,1:T(8,128)S(1)} %add_bitcast_fusion) | data formatting | bytes 3145728 | tf_op jit(solution)/shard_map/add | solution.py:133
  120.6 31.3 %reduce-scatter.2.cloned.1.call-done = f32[3,256,128]{2,1,0:T(8,128)} async-done(((f32[3,256,512]{2,1,0:T(8,128)}), f32[3,256,128]{2,1,0:T(8,128)}) %reduce-scatter.2.cloned.1.call-update) | async-done | bytes 393232 | tf_op jit(solution)/shard_map/reduce_scatter | solution.py:134
  (76 shorter events, 4.9 us)
Async XLA Ops:
  6.5 111.8 %copy-start = (bf16[1,16,32,768]{3,2,1,0:T(8,128)(2,1)S(1)}, bf16[1,16,32,768]{3,2,1,0:T(8,128)(2,1)}, u32[]{:S(2)}) copy-start(bf16[1,16,32,768]{3,2,1,0:T(8,128)(2,1)} %param.17) | copy-start | bytes 2359300
  6.5 6.3 %copy-start.6 = (s32[256]{0:T(256)S(1)}, s32[256]{0:T(256)}, u32[]{:S(2)}) copy-start(s32[256]{0:T(256)} %param.13) | copy-start | bytes 3076
  6.5 9.2 %copy-start.1 = (bf16[3,256,512]{2,1,0:T(8,128)(2,1)S(1)}, bf16[3,256,512]{2,1,0:T(8,128)(2,1)}, u32[]{:S(2)}) copy-start(bf16[3,256,512]{2,1,0:T(8,128)(2,1)} %param.12) | copy-start | bytes 2359300
  6.5 7.2 %copy-start.3 = (bf16[2,32,3,256]{3,1,2,0:T(8,128)(2,1)S(1)}, bf16[2,32,3,256]{3,1,2,0:T(8,128)(2,1)}, u32[]{:S(2)}) copy-start(bf16[2,32,3,256]{3,1,2,0:T(8,128)(2,1)} %param.14) | copy-start | bytes 294916
  6.5 97.1 %all-reduce.2.cloned.1.call-start = ((), (), s32[]{:S(2)}) async-start(), calls=%async_computation.1 | async-start | bytes 1048576 | tf_op jit(solution)/shard_map/psum | solution.py:112
  6.6 7.6 %collective-permute-start = (s32[256]{0:T(256)}, s32[256]{0:T(256)S(1)}, u32[]{:S(2)}, u32[]{:S(2)}) collective-permute-start(s32[256]{0:T(256)} %param.13), channel_id=1, source_target_pairs={{1,0},{2,1},{3,2},{4,3},{5,4},{6,5},{7,6},{0,7},{9,8},{10,9},{11,1... | collective-permute-start | bytes 3080 | tf_op jit(solution)/shard_map/ppermute | solution.py:16
  7.3 7.5 %collective-permute-start.2 = (s32[256]{0:T(256)}, s32[256]{0:T(256)S(1)}, u32[]{:S(2)}, u32[]{:S(2)}) collective-permute-start(s32[256]{0:T(256)} %param.13), channel_id=1, source_target_pairs={{0,1},{1,2},{2,3},{3,4},{4,5},{5,6},{6,7},{7,0},{8,9},{9,10},{10,1... | collective-permute-start | bytes 3080 | tf_op jit(solution)/shard_map/ppermute | solution.py:14
  14.1 17.2 %copy-start.4 = (pred[256]{0:T(512)(128)(4,1)}, pred[256]{0:T(512)(128)(4,1)S(1)}, u32[]{:S(2)}) copy-start(pred[256]{0:T(512)(128)(4,1)S(1)} %get-tuple-element.6) | copy-start | bytes 772
  17.0 3.1 %collective-permute-start.1 = (bf16[3,64,512]{2,1,0:T(8,128)(2,1)S(1)}, bf16[3,64,512]{2,1,0:T(8,128)(2,1)S(1)}, u32[]{:S(2)}, u32[]{:S(2)}) collective-permute-start(bf16[3,64,512]{2,1,0:T(8,128)(2,1)S(1)} %select_bitcast_fusion.2), channel_id=1, source_target_pairs={{0,1},{1,2},{2,3},{3,4},{4,5},{5,6},{6,7},{7,0},{8,9},{9,10},{10,1... | collective-permute-start | bytes 589832 | tf_op jit(solution)/shard_map/ppermute | solution.py:25
  18.8 7.3 %collective-permute-start.3 = (bf16[3,64,512]{2,1,0:T(8,128)(2,1)S(1)}, bf16[3,64,512]{2,1,0:T(8,128)(2,1)S(1)}, u32[]{:S(2)}, u32[]{:S(2)}) collective-permute-start(bf16[3,64,512]{2,1,0:T(8,128)(2,1)S(1)} %select_bitcast_fusion.1), channel_id=1, source_target_pairs={{0,7},{1,0},{2,1},{3,2},{4,3},{5,4},{6,5},{7,6},{8,15},{9,8},{10,9... | collective-permute-start | bytes 589832 | tf_op jit(solution)/shard_map/ppermute | solution.py:25
  32.5 74.2 %collective-permute-start.4 = (bf16[3,256,512]{2,1,0:T(8,128)(2,1)S(1)}, bf16[3,256,512]{2,1,0:T(8,128)(2,1)S(1)}, u32[]{:S(2)}, u32[]{:S(2)}) collective-permute-start(bf16[3,256,512]{2,1,0:T(8,128)(2,1)S(1)} %copy.46), channel_id=1, source_target_pairs={{0,2},{1,3},{2,4},{3,5},{4,6},{5,7},{6,0},{7,1},{8,10},{9,11},{10,... | collective-permute-start | bytes 2359304 | tf_op jit(solution)/shard_map/ppermute | solution.py:25
  33.4 72.0 %copy-start.2 = (bf16[1,16,32,32]{3,2,1,0:T(8,128)(2,1)S(1)}, bf16[1,16,32,32]{3,2,1,0:T(8,128)(2,1)}, u32[]{:S(2)}) copy-start(bf16[1,16,32,32]{3,2,1,0:T(8,128)(2,1)} %param.18) | copy-start | bytes 98308
  34.5 117.4 %reduce-scatter.2.cloned.1.call-start = ((), (), s32[]{:S(2)}) async-start(), calls=%async_computation.2 | async-start | bytes 1966080 | tf_op jit(solution)/shard_map/reduce_scatter | solution.py:134
  35.2 72.2 %collective-permute-start.5 = (bf16[3,256,512]{2,1,0:T(8,128)(2,1)S(1)}, bf16[3,256,512]{2,1,0:T(8,128)(2,1)}, u32[]{:S(2)}, u32[]{:S(2)}) collective-permute-start(bf16[3,256,512]{2,1,0:T(8,128)(2,1)S(1)} %copy.46), channel_id=1, source_target_pairs={{0,1},{1,2},{2,3},{3,4},{4,5},{5,6},{6,7},{7,0},{8,9},{9,10},{10,1... | collective-permute-start | bytes 2359304 | tf_op jit(solution)/shard_map/ppermute | solution.py:25
  35.3 75.2 %collective-permute-start.6 = (bf16[3,256,512]{2,1,0:T(8,128)(2,1)S(1)}, bf16[3,256,512]{2,1,0:T(8,128)(2,1)}, u32[]{:S(2)}, u32[]{:S(2)}) collective-permute-start(bf16[3,256,512]{2,1,0:T(8,128)(2,1)S(1)} %copy.46), channel_id=1, source_target_pairs={{0,7},{1,0},{2,1},{3,2},{4,3},{5,4},{6,5},{7,6},{8,15},{9,8},{10,9... | collective-permute-start | bytes 2359304 | tf_op jit(solution)/shard_map/ppermute | solution.py:25
  35.7 76.7 %collective-permute-start.7 = (bf16[3,256,512]{2,1,0:T(8,128)(2,1)S(1)}, bf16[3,256,512]{2,1,0:T(8,128)(2,1)}, u32[]{:S(2)}, u32[]{:S(2)}) collective-permute-start(bf16[3,256,512]{2,1,0:T(8,128)(2,1)S(1)} %copy.46), channel_id=1, source_target_pairs={{0,6},{1,7},{2,0},{3,1},{4,2},{5,3},{6,4},{7,5},{8,14},{9,15},{10,... | collective-permute-start | bytes 2359304 | tf_op jit(solution)/shard_map/ppermute | solution.py:25
  103.6 1.8 %copy-start.7 = (f32[1,16]{1,0:T(1,128)S(1)}, f32[1,16]{1,0:T(1,128)}, u32[]{:S(2)}) copy-start(f32[1,16]{1,0:T(1,128)} %param.19) | copy-start | bytes 196
  106.7 2.6 %copy-start.5 = (pred[256]{0:T(512)(128)(4,1)S(1)}, pred[256]{0:T(512)(128)(4,1)}, u32[]{:S(2)}) copy-start(pred[256]{0:T(512)(128)(4,1)} %copy-done.4) | copy-start | bytes 772
  115.0 1.7 %copy-start.8 = (bf16[1,2,768,768]{3,2,1,0:T(8,128)(2,1)S(1)}, bf16[1,2,768,768]{3,2,1,0:T(8,128)(2,1)}, u32[]{:S(2)}) copy-start(bf16[1,2,768,768]{3,2,1,0:T(8,128)(2,1)} %param.15) | copy-start | bytes 7077892
Sparse Core Ops, SparseCore 0:
  34.6 68.9 all-reduce.1
  120.8 31.0 reduce-scatter.1
where the time goes:
time: 161 us; the launch traced here: 159 us
  waiting for transfers between devices  105 us (65%)
  local copies, waits for them, and re-layouts  20.4 us (13%)
  between operations  15.1 us (9%)
  other arithmetic  7.89 us (5%)
  matrix products  5.57 us (3%)
  starting transfers between devices  4.69 us (3%)
    psum x1, waiting for transfers between devices, on_device(): table = lax.psum(table, 'clu')  66.9 us
    reduce_scatter x1, waiting for transfers between devices, on_device(): lax.psum_scatter(partial_value, 'grp', scatter_dimension=2, tiled=True)  31.3 us
    unnamed x25, local copies, waits for them, and re-layouts  8.73 us
    ppermute x6, waiting for transfers between devices, from_behind(): lax.ppermute(shard, axis, [(i, (i + by) % size) for i in range(size)])  6.96 us
  transfers between devices with their start and end apart: 10, of which 4 were waited for; matrix products, arithmetic and copies ran while one was open for 11% of the time, Pallas kernels for 0%

commit v1 on v0

v1 whole, which is shorter than its diff:
```python
import functools

import jax
import jax.numpy as jnp
from jax import lax
from jax.experimental import pallas as pl
from jax.experimental.pallas import tpu as pltpu
from jax.sharding import PartitionSpec as P

MESH = pl.DeviceIdType.MESH
F32, BF16 = jnp.float32, jnp.bfloat16


def kernel(
    n, groups, levels, rank,
    forces, order, bases, tiles_hbm, near_col, basis_hbm, coupling, scale, ranks, targets,
    out,
    raw, ext, ext_out, orders, tiles, basis, spread, picks, own_pick, piece_out, pieces,
    table_out, tables, coupled, total, y_out, y_in,
    local_sem, order_send, order_recv, raw_send, raw_recv, ext_send, ext_recv,
    piece_send, piece_recv, table_send, table_recv, y_send, y_recv,
):
    g, c = lax.axis_index("grp"), lax.axis_index("clu")
    core = lax.rem(c, 2)
    comps, tile, columns = forces.shape
    width = columns // groups
    quarter = tile // 4
    slots = raw.shape[1]
    rows = comps * tile
    near_count = tiles.shape[0]
    far_count = targets.shape[1]
    coarse = 2 ** (levels + 1) - 2

    def at_clu(by):
        return {"grp": g, "clu": lax.rem(c + by + n, n)}

    def at_grp(by):
        return {"grp": lax.rem(g + by, groups), "clu": c}

    mate = {"grp": g, "clu": c + 1 - 2 * core}

    def remote(src, dst, send, recv, where):
        return pltpu.make_async_remote_copy(
            src_ref=src, dst_ref=dst, send_sem=send, recv_sem=recv, device_id=where, device_id_type=MESH
        )

    def own_columns(i):
        q = lax.rem(g + i, groups)
        return forces.at[:, :, pl.ds(pl.multiple_of(q * width, width), width)]

    local = [pltpu.make_async_copy(own_columns(i), raw.at[i, 2 + core], local_sem.at[i]) for i in range(groups)]
    for copy in local:
        copy.start()
    tiles_copy = pltpu.make_async_copy(tiles_hbm, tiles, local_sem.at[groups])
    basis_copy = pltpu.make_async_copy(basis_hbm, basis, local_sem.at[groups + 1])
    tiles_copy.start()
    basis_copy.start()

    barrier = pltpu.get_barrier_semaphore()

    def greet(d, carry):
        pl.semaphore_signal(barrier, inc=1, device_id=at_clu(d), device_id_type=MESH)
        return carry

    lax.fori_loop(1, n, greet, 0)
    for d in range(1, groups):
        pl.semaphore_signal(barrier, inc=1, device_id=at_grp(d), device_id_type=MESH)
    pl.semaphore_wait(barrier, n - 1 + groups - 1)

    sends = []
    offsets = (-2, -1, 1, 2)
    order_copies = []
    for at, by in enumerate(offsets):
        copy = remote(order, orders.at[2 - by], order_send.at[at], order_recv.at[2 - by], at_clu(by))
        copy.start()
        order_copies.append(copy)

    def send_raw(i):
        group = [
            remote(own_columns(i), raw.at[i, core], raw_send.at[i, 0], raw_recv.at[i, core], at_clu(2)),
            remote(own_columns(i), raw.at[i, 4 + core], raw_send.at[i, 1], raw_recv.at[i, 4 + core], at_clu(-2)),
            remote(own_columns(i), raw.at[i, 2 + core], raw_send.at[i, 2], raw_recv.at[i, 2 + core], mate),
        ]
        for copy in group:
            copy.start()
            sends.append(copy)

    def arrived(i, slot):
        remote(raw.at[i, slot], raw.at[i, slot], raw_send.at[i, 0], raw_recv.at[i, slot], mate).wait_recv()

    def take_raw(i):
        for at, slot in ((3, core), (4, 4 + core)):
            arrived(i, slot)
            copy = remote(raw.at[i, slot], raw.at[i, slot], raw_send.at[i, at], raw_recv.at[i, slot], mate)
            copy.start()
            sends.append(copy)
        for slot in (3 - core, 1 - core, 5 - core):
            arrived(i, slot)

    send_raw(0)
    send_raw(1)

    lane = lax.broadcasted_iota(jnp.int32, (rank, coarse * rank), 1)
    row = lax.broadcasted_iota(jnp.int32, (rank, coarse * rank), 0)
    repeat = (lax.rem(lane, rank) == row).astype(BF16)
    wide = jnp.dot(coupling[...], repeat, preferred_element_type=F32)
    for b in range(far_count):
        start = targets[0, b] * rank
        keep = (lane >= start) & (lane < start + ranks[0, b])
        spread[b * rank:(b + 1) * rank, :] = jnp.where(keep, wide[b * rank:(b + 1) * rank, :], 0.0).astype(BF16)
    ext[quarter:, :] = jnp.zeros((ext.shape[0] - quarter, ext.shape[1]), BF16)

    sub = lax.broadcasted_iota(jnp.int32, (tile, tile), 0)
    lan = lax.broadcasted_iota(jnp.int32, (tile, tile), 1)
    upto = (sub <= lan).astype(BF16)
    first = (c - core - 2) * tile

    def ranked(chosen):
        spots = jnp.broadcast_to(chosen.astype(F32), (8, tile)).astype(BF16)
        return (jnp.dot(spots, upto, preferred_element_type=F32)[0:1, :] - 1.0).astype(jnp.int32)

    def one_hot(cluster_order, dst):
        spot = cluster_order - first
        spot = jnp.where(spot < 0, spot + n * tile, spot)
        spot = jnp.where(spot >= n * tile, spot - n * tile, spot)
        beyond = spot >= slots * tile
        spot = jnp.where(beyond, slots * tile + ranked(beyond), spot)
        down = jnp.broadcast_to(spot.astype(F32), (128, tile)).T
        at = lax.broadcasted_iota(jnp.int32, (tile, 128), 1).astype(F32)
        for j in range(dst.shape[1] // 128):
            dst[:, j * 128:(j + 1) * 128] = (down == at + float(j * 128)).astype(F32).astype(BF16)

    one_hot(order[...], own_pick)
    for copy in local:
        copy.wait()
    for at, by in enumerate(offsets):
        order_copies[at].wait_send()
        remote(orders.at[2 + by], orders.at[2 + by], order_send.at[at], order_recv.at[2 + by], mate).wait_recv()
    orders[2] = order[...]

    away = orders[1 + 2 * core] - c * tile
    chosen = (away >= 0) & (away < tile)
    place = jnp.where(chosen, ranked(chosen), -1)
    left = (lax.broadcasted_iota(jnp.int32, (ext.shape[0], tile), 0) == place).astype(F32).astype(BF16)
    right = (sub == away).astype(F32).astype(BF16)
    pick = lax.dot_general(left, right, (((1,), (1,)), ((), ())), preferred_element_type=F32).astype(BF16)
    for i in range(groups):
        block = jnp.concatenate([raw[i, 2 + core, d] for d in range(comps)], axis=1)
        got = jnp.dot(pick, block, preferred_element_type=F32).astype(BF16)
        ext_out[:, i * comps * width:(i + 1) * comps * width] = got[:quarter]
    ext_copy = remote(ext_out, ext.at[0:quarter], ext_send.at[0], ext_recv.at[0], at_clu(6 * core - 3))
    ext_copy.start()

    def gathered(pick_ref, i, with_ext):
        block = jnp.concatenate([raw[i, :, d].reshape(slots * tile, width) for d in range(comps)], axis=1)
        x = jnp.dot(pick_ref[:, :slots * tile], block, preferred_element_type=F32)
        if with_ext:
            x = x + jnp.dot(
                pick_ref[:, slots * tile:], ext[:, i * comps * width:(i + 1) * comps * width],
                preferred_element_type=F32,
            )
        x = x.astype(BF16)
        return jnp.concatenate([x[:, d * width:(d + 1) * width] for d in range(comps)], axis=0)

    take_raw(0)
    piece = jnp.dot(bases[...], gathered(own_pick, 0, False), preferred_element_type=F32)
    piece_out[...] = piece

    def piece_copy(d):
        return remote(piece_out, pieces.at[c], piece_send.at[d], piece_recv.at[c], at_clu(d))

    def start_piece(d, carry):
        piece_copy(d).start()
        return carry

    lax.fori_loop(1, n, start_piece, 0)
    pieces[c] = piece
    for i in range(2, groups):
        send_raw(i)

    for j in range(near_count):
        spot = near_col[0, j] - c + 2
        spot = jnp.where(spot < 0, spot + n, spot)
        spot = jnp.where(spot >= n, spot - n, spot)
        one_hot(orders[jnp.clip(spot, 0, 4)], picks.at[j])
    tiles_copy.wait()
    basis_copy.wait()

    def near(i):
        part = jnp.zeros((rows, width), F32)
        for j in range(near_count):
            part = part + jnp.dot(tiles[j], gathered(picks.at[j], i, True), preferred_element_type=F32)
        total[i] = part

    def send_y(i):
        y_out[i] = total[i].astype(BF16)
        copy = remote(y_out.at[i], y_in.at[i], y_send.at[i], y_recv.at[i], at_grp(i))
        copy.start()
        sends.append(copy)

    take_raw(1)
    ext_copy.wait_recv()
    near(1)

    def await_piece(d, carry):
        source = lax.rem(c + d, n)
        remote(piece_out, pieces.at[source], piece_send.at[d], piece_recv.at[source], at_clu(d)).wait_recv()
        return carry

    lax.fori_loop(1, n, await_piece, 0)
    for level in range(levels):
        count = 2 ** (level + 1)
        members = n // count
        for k in range(count):
            entry = lax.fori_loop(
                0, members,
                lambda m, acc, k=k, members=members, level=level: acc
                + pieces[k * members + m, level * rank:(level + 1) * rank, :],
                jnp.zeros((rank, width), F32),
            )
            at = (count - 2 + k) * rank
            table_out[at:at + rank, :] = entry
            tables[0, at:at + rank, :] = entry
    for d in range(1, groups):
        copy = remote(table_out, tables.at[groups - d], table_send.at[d], table_recv.at[groups - d], at_grp(d))
        copy.start()
        sends.append(copy)
    near(0)
    for i in range(2, groups - 1):
        take_raw(i)
        near(i)

    for d in range(1, groups):
        remote(table_out, tables.at[d], table_send.at[d], table_recv.at[d], at_grp(d)).wait_recv()
    table = jnp.concatenate([tables[i] for i in range(groups)], axis=1)
    high = table.astype(BF16)
    low = (table - high.astype(F32)).astype(BF16)
    mixed = jnp.dot(spread[...], high, preferred_element_type=F32)
    mixed = mixed + jnp.dot(spread[...], low, preferred_element_type=F32)
    for b in range(far_count):
        coupled[b * rank:(b + 1) * rank, :] = (mixed[b * rank:(b + 1) * rank, :] * scale[0, b]).astype(BF16)
    far = lax.dot_general(basis[...], coupled[...], (((0,), (0,)), ((), ())), preferred_element_type=F32)
    for i in range(groups - 1):
        total[i] = total[i] + far[:, i * width:(i + 1) * width]
    total[groups - 1] = far[:, (groups - 1) * width:]
    for i in range(1, groups - 1):
        send_y(i)
    last = groups - 1
    far_part = total[last]
    take_raw(last)
    near(last)
    total[last] = total[last] + far_part
    send_y(last)

    answer = total[0]
    for i in range(1, groups):
        remote(y_out.at[i], y_in.at[i], y_send.at[i], y_recv.at[i], at_grp(i)).wait_recv()
        answer = answer + y_in[i].astype(F32)
    out[...] = answer.reshape(comps, tile, width)

    for copy in sends:
        copy.wait_send()
    ext_copy.wait_send()

    def end_piece(d, carry):
        piece_copy(d).wait_send()
        return carry

    lax.fori_loop(1, n, end_piece, 0)


def solution(mesh):
    n, groups = mesh.shape["clu"], mesh.shape["grp"]

    def on_device(forces, order, bases, near_tiles, near_col, far_basis, far_coupling, far_scale, far_rank, far_target):
        comps, tile, columns = forces.shape
        levels, rank = bases.shape[:2]
        near_count, far_count = near_tiles.shape[1], far_basis.shape[1]
        width, rows, quarter = columns // groups, comps * tile, tile // 4
        coarse = 2 ** (levels + 1) - 2
        slots = 6
        pad = 128
        vmem, smem, hbm = (pl.BlockSpec(memory_space=m) for m in (pltpu.VMEM, pltpu.SMEM, pl.ANY))
        dma = pltpu.SemaphoreType.DMA
        return pl.pallas_call(
            functools.partial(kernel, n, groups, levels, rank),
            out_shape=jax.ShapeDtypeStruct((comps, tile, width), F32),
            in_specs=[hbm, vmem, vmem, hbm, smem, hbm, vmem, smem, smem, smem],
            out_specs=vmem,
            scratch_shapes=[
                pltpu.VMEM((groups, slots, comps, tile, width), BF16),
                pltpu.VMEM((pad, comps * columns), BF16),
                pltpu.VMEM((quarter, comps * columns), BF16),
                pltpu.VMEM((5, 1, tile), jnp.int32),
                pltpu.VMEM((near_count, rows, rows), BF16),
                pltpu.VMEM((far_count * rank, rows), BF16),
                pltpu.VMEM((far_count * rank, coarse * rank), BF16),
                pltpu.VMEM((near_count, tile, slots * tile + pad), BF16),
                pltpu.VMEM((tile, slots * tile), BF16),
                pltpu.VMEM((levels * rank, width), F32),
                pltpu.VMEM((n, levels * rank, width), F32),
                pltpu.VMEM((coarse * rank, width), F32),
                pltpu.VMEM((groups, coarse * rank, width), F32),
                pltpu.VMEM((far_count * rank, columns), BF16),
                pltpu.VMEM((groups, rows, width), F32),
                pltpu.VMEM((groups, rows, width), BF16),
                pltpu.VMEM((groups, rows, width), BF16),
                dma((groups + 2,)),
                dma((4,)), dma((5,)),
                dma((groups, 5)), dma((groups, slots)),
                dma((1,)), dma((1,)),
                dma((n,)), dma((n,)),
                dma((groups,)), dma((groups,)),
                dma((groups,)), dma((groups,)),
            ],
            compiler_params=pltpu.CompilerParams(
                collective_id=0, has_side_effects=True, vmem_limit_bytes=60 * 1024 * 1024
            ),
        )(
            forces,
            order.reshape(1, tile),
            bases.reshape(levels * rank, rows),
            near_tiles.reshape(near_count, rows, rows),
            near_col,
            far_basis.reshape(far_count * rank, rows),
            far_coupling.reshape(far_count * rank, rank),
            far_scale,
            far_rank,
            far_target,
        )

    placed = (
        P(None, "clu", None),
        P("clu"),
        P(None, None, None, "clu"),
        P("clu", "grp", None, None),
        P("clu", "grp"),
        P("clu", "grp", None, None),
        P("clu", "grp", None, None),
        P("clu", "grp"),
        P("clu", "grp"),
        P("clu", "grp"),
    )
    return jax.shard_map(
        on_device, mesh=mesh, in_specs=placed, out_specs=P(None, "clu", "grp"), check_vma=False
    )
```

time: 161 us -> 71.3 us (0.44); the launches traced: 159 us -> 71.1 us
  waiting for transfers between devices: 105 us -> 0 us
  Pallas kernels: 0 us -> 67.7 us
  local copies, waits for them, and re-layouts: 20.4 us -> 3.4 us
  between operations: 15.1 us -> 0.01 us
  other arithmetic: 7.89 us -> 0 us
  matrix products: 5.57 us -> 0 us
  starting transfers between devices: 4.69 us -> 0 us
    pallas_call x0 -> x1, Pallas kernels: none -> 67.7 us  [on_device(): pl.pallas_call(functools.partial(kernel, n, groups, levels, rank), out_sh...]
    psum x1 -> x0, waiting for transfers between devices: 66.9 us -> none  [on_device(): table = lax.psum(table, 'clu')]
    reduce_scatter x1 -> x0, waiting for transfers between devices: 31.3 us -> none  [on_device(): lax.psum_scatter(partial_value, 'grp', scatter_dimension=2, tiled=True)]
    ppermute x8 -> x0, waiting for transfers between devices: 6.97 us -> none  [the longest x6 6.96 us: from_behind(): lax.ppermute(shard, axis, [(i, (i + by) % size) for i in range(size)])]
    dot_general x6 -> x0, matrix products: 5.57 us -> none  [the longest x1 1.75 us: on_device(): jnp.dot(selector, table.reshape(coarse_count, rank * columns), precision=...]
    unnamed x25 -> x3, local copies, waits for them, and re-layouts: 8.73 us -> 3.4 us
    gather x3 -> x0, local copies, waits for them, and re-layouts: 5.32 us -> none  [the longest x1 2.94 us: nearby_forces(): own_block = jnp.take(stacked, positions, axis=1)]
    ppermute x8 -> x0, starting transfers between devices: 4.62 us -> none  [the longest x6 2.64 us: from_behind(): lax.ppermute(shard, axis, [(i, (i + by) % size) for i in range(size)])]
  transfers between devices with their start and end apart: 10 -> 0, of which waited for: 4 -> 0; matrix products, arithmetic and copies ran while one was open for 11% -> 0% of each run, Pallas kernels for 0% -> 0%
where the time goes in v1:
time: 71.3 us; the launch traced here: 71.1 us
  Pallas kernels  67.7 us (95%)
  local copies, waits for them, and re-layouts  3.4 us (5%)
    pallas_call x1, Pallas kernels, on_device(): pl.pallas_call(functools.partial(kernel, n, groups, levels, rank), out_sh...  67.7 us
    unnamed x3, local copies, waits for them, and re-layouts  3.4 us

profile of v1, /device:TPU:9, one launch (start us, length us, event | category | flops | bytes accessed | tf_op | source)
XLA Modules:
  0.0 71.1 jit_solution(16582716667472274638)
XLA Ops:
  0.0 1.0 %copy.12 = bf16[2,32,3,256]{3,2,1,0:T(4,128)(2,1)S(1)} copy(bf16[2,32,3,256]{3,1,2,0:T(8,128)(2,1)} %param.12) | data formatting | bytes 196608 | tf_op args[2]
  1.0 0.7 copy.13
  1.6 67.7 %shard_map.100 = f32[3,256,128]{2,1,0:T(8,128)} custom-call(bf16[3,256,512]{2,1,0:T(8,128)(2,1)} %forces.1, s32[1,256]{1,0:T(1,128)} %bitcast.12, bf16[64,768]{1,0:T(8,128)(2,1)} %bitcast.10, bf16[2,768,768]{2,1,0:T(8,128)(2,1)} %bitcast.7, s32[1,2]{1,0:T(1,128)} %near_col.1, bf16[512,768]{1,0:T(8,128)(2,1)} %bitcast.8, bf16[512,32]{1,0:T(8,128)(2,1)} %bitcast.11, ...), custom_call_target="tpu_custom_call" | custom-call | tf_op jit(solution)/shard_map/pallas_call | solution.py:285
  69.4 1.8 %copy.15 = f32[3,256,128]{2,1,0:T(8,128)} copy(f32[3,256,128]{2,1,0:T(8,128)} %shard_map.100) | data formatting | bytes 786432

commit v2 on v1

--- a/solution.py
+++ b/solution.py
@@ -15,7 +15,7 @@
     n, groups, levels, rank,
     forces, order, bases, tiles_hbm, near_col, basis_hbm, coupling, scale, ranks, targets,
     out,
-    raw, ext, ext_out, orders, tiles, basis, spread, picks, own_pick, piece_out, pieces,
+    raw, ext, ext_out, orders, tiles, basis, spread, picks, own_pick, piece_out, piece_mate, pieces,
     table_out, tables, coupled, total, y_out, y_in,
     local_sem, order_send, order_recv, raw_send, raw_recv, ext_send, ext_recv,
     piece_send, piece_recv, table_send, table_recv, y_send, y_recv,
@@ -30,12 +30,15 @@
     near_count = tiles.shape[0]
     far_count = targets.shape[1]
     coarse = 2 ** (levels + 1) - 2
+    half = n // 2
 
     def at_clu(by):
         return {"grp": g, "clu": lax.rem(c + by + n, n)}
 
-    def at_grp(by):
-        return {"grp": lax.rem(g + by, groups), "clu": c}
+    partners = (g, g + 1 - 2 * lax.rem(g, 2), lax.rem(g + 2, groups), groups - 1 - g)
+
+    def at_grp(i):
+        return {"grp": partners[i], "clu": c}
 
     mate = {"grp": g, "clu": c + 1 - 2 * core}
 
@@ -45,7 +48,7 @@
         )
 
     def own_columns(i):
-        q = lax.rem(g + i, groups)
+        q = partners[i]
         return forces.at[:, :, pl.ds(pl.multiple_of(q * width, width), width)]
 
     local = [pltpu.make_async_copy(own_columns(i), raw.at[i, 2 + core], local_sem.at[i]) for i in range(groups)]
@@ -68,6 +71,7 @@
     pl.semaphore_wait(barrier, n - 1 + groups - 1)
 
     sends = []
+    near_groups, far_group = range(1, groups - 1), groups - 1
     offsets = (-2, -1, 1, 2)
     order_copies = []
     for at, by in enumerate(offsets):
@@ -79,18 +83,29 @@
         group = [
             remote(own_columns(i), raw.at[i, core], raw_send.at[i, 0], raw_recv.at[i, core], at_clu(2)),
             remote(own_columns(i), raw.at[i, 4 + core], raw_send.at[i, 1], raw_recv.at[i, 4 + core], at_clu(-2)),
-            remote(own_columns(i), raw.at[i, 2 + core], raw_send.at[i, 2], raw_recv.at[i, 2 + core], mate),
         ]
         for copy in group:
             copy.start()
             sends.append(copy)
 
+    def send_mate(i):
+        copy = remote(own_columns(i), raw.at[i, 2 + core], raw_send.at[i, 2], raw_recv.at[i, 2 + core], mate)
+        copy.start()
+        sends.append(copy)
+
     def arrived(i, slot):
         remote(raw.at[i, slot], raw.at[i, slot], raw_send.at[i, 0], raw_recv.at[i, slot], mate).wait_recv()
 
     def take_raw(i):
         for at, slot in ((3, core), (4, 4 + core)):
             arrived(i, slot)
+            if i == 0:
+                for to in near_groups:
+                    across = remote(
+                        raw.at[0, slot], raw.at[to, slot], raw_send.at[to, at - 3], raw_recv.at[to, slot], at_grp(to)
+                    )
+                    across.start()
+                    sends.append(across)
             copy = remote(raw.at[i, slot], raw.at[i, slot], raw_send.at[i, at], raw_recv.at[i, slot], mate)
             copy.start()
             sends.append(copy)
@@ -98,7 +113,8 @@
             arrived(i, slot)
 
     send_raw(0)
-    send_raw(1)
+    for i in range(groups):
+        send_mate(i)
 
     lane = lax.broadcasted_iota(jnp.int32, (rank, coarse * rank), 1)
     row = lax.broadcasted_iota(jnp.int32, (rank, coarse * rank), 0)
@@ -108,7 +124,7 @@
         start = targets[0, b] * rank
         keep = (lane >= start) & (lane < start + ranks[0, b])
         spread[b * rank:(b + 1) * rank, :] = jnp.where(keep, wide[b * rank:(b + 1) * rank, :], 0.0).astype(BF16)
-    ext[quarter:, :] = jnp.zeros((ext.shape[0] - quarter, ext.shape[1]), BF16)
+    ext[:, quarter:, :] = jnp.zeros((groups, ext.shape[1] - quarter, ext.shape[2]), BF16)
 
     sub = lax.broadcasted_iota(jnp.int32, (tile, tile), 0)
     lan = lax.broadcasted_iota(jnp.int32, (tile, tile), 1)
@@ -141,42 +157,56 @@
     away = orders[1 + 2 * core] - c * tile
     chosen = (away >= 0) & (away < tile)
     place = jnp.where(chosen, ranked(chosen), -1)
-    left = (lax.broadcasted_iota(jnp.int32, (ext.shape[0], tile), 0) == place).astype(F32).astype(BF16)
+    left = (lax.broadcasted_iota(jnp.int32, (ext.shape[1], tile), 0) == place).astype(F32).astype(BF16)
     right = (sub == away).astype(F32).astype(BF16)
     pick = lax.dot_general(left, right, (((1,), (1,)), ((), ())), preferred_element_type=F32).astype(BF16)
-    for i in range(groups):
+    for at, i in enumerate((0, far_group)):
         block = jnp.concatenate([raw[i, 2 + core, d] for d in range(comps)], axis=1)
-        got = jnp.dot(pick, block, preferred_element_type=F32).astype(BF16)
-        ext_out[:, i * comps * width:(i + 1) * comps * width] = got[:quarter]
-    ext_copy = remote(ext_out, ext.at[0:quarter], ext_send.at[0], ext_recv.at[0], at_clu(6 * core - 3))
-    ext_copy.start()
+        ext_out[at] = jnp.dot(pick, block, preferred_element_type=F32).astype(BF16)[:quarter]
+        copy = remote(
+            ext_out.at[at], ext.at[i, 0:quarter], ext_send.at[i], ext_recv.at[i], at_clu(6 * core - 3)
+        )
+        copy.start()
+        sends.append(copy)
+
+    def take_ext(i):
+        rows_in = ext.at[i, 0:quarter]
+        remote(rows_in, rows_in, ext_send.at[i], ext_recv.at[i], mate).wait_recv()
 
     def gathered(pick_ref, i, with_ext):
         block = jnp.concatenate([raw[i, :, d].reshape(slots * tile, width) for d in range(comps)], axis=1)
         x = jnp.dot(pick_ref[:, :slots * tile], block, preferred_element_type=F32)
         if with_ext:
             x = x + jnp.dot(
-                pick_ref[:, slots * tile:], ext[:, i * comps * width:(i + 1) * comps * width],
-                preferred_element_type=F32,
+                pick_ref[:, slots * tile:], ext[i], preferred_element_type=F32
             )
         x = x.astype(BF16)
         return jnp.concatenate([x[:, d * width:(d + 1) * width] for d in range(comps)], axis=0)
 
     take_raw(0)
-    piece = jnp.dot(bases[...], gathered(own_pick, 0, False), preferred_element_type=F32)
-    piece_out[...] = piece
+    own_rows = gathered(own_pick, 0, False)
+    piece = jnp.zeros((levels * rank, width), F32)
+    for d in range(comps):
+        part = jnp.concatenate([bases[level, d] for level in range(levels)], axis=0)
+        piece = piece + jnp.dot(part, own_rows[d * tile:(d + 1) * tile], preferred_element_type=F32)
+    piece_out[0] = piece
+    copy = remote(piece_out.at[0], piece_mate, piece_send.at[0], piece_recv.at[half], mate)
+    copy.start()
+    sends.append(copy)
+    copy.wait_recv()
+    pair = piece + piece_mate[...]
+    piece_out[1] = pair
+    pieces[c // 2] = pair
 
     def piece_copy(d):
-        return remote(piece_out, pieces.at[c], piece_send.at[d], piece_recv.at[c], at_clu(d))
+        return remote(piece_out.at[1], pieces.at[c // 2], piece_send.at[d], piece_recv.at[c // 2], at_clu(2 * d))
 
     def start_piece(d, carry):
         piece_copy(d).start()
         return carry
 
-    lax.fori_loop(1, n, start_piece, 0)
-    pieces[c] = piece
-    for i in range(2, groups):
-        send_raw(i)
+    lax.fori_loop(1, half, start_piece, 0)
+    send_raw(far_group)
 
     for j in range(near_count):
         spot = near_col[0, j] - c + 2
@@ -198,19 +228,23 @@
         copy.start()
         sends.append(copy)
 
-    take_raw(1)
-    ext_copy.wait_recv()
-    near(1)
+    take_ext(0)
+    for to in near_groups:
+        across = remote(
+            ext.at[0, 0:quarter], ext.at[to, 0:quarter], ext_send.at[to], ext_recv.at[to], at_grp(to)
+        )
+        across.start()
+        sends.append(across)
 
     def await_piece(d, carry):
-        source = lax.rem(c + d, n)
-        remote(piece_out, pieces.at[source], piece_send.at[d], piece_recv.at[source], at_clu(d)).wait_recv()
+        source = lax.rem(c // 2 + d, half)
+        remote(piece_out.at[1], pieces.at[source], piece_send.at[d], piece_recv.at[source], mate).wait_recv()
         return carry
 
-    lax.fori_loop(1, n, await_piece, 0)
+    lax.fori_loop(1, half, await_piece, 0)
     for level in range(levels):
         count = 2 ** (level + 1)
-        members = n // count
+        members = half // count
         for k in range(count):
             entry = lax.fori_loop(
                 0, members,
@@ -222,12 +256,13 @@
             table_out[at:at + rank, :] = entry
             tables[0, at:at + rank, :] = entry
     for d in range(1, groups):
-        copy = remote(table_out, tables.at[groups - d], table_send.at[d], table_recv.at[groups - d], at_grp(d))
+        copy = remote(table_out, tables.at[d], table_send.at[d], table_recv.at[d], at_grp(d))
         copy.start()
         sends.append(copy)
     near(0)
-    for i in range(2, groups - 1):
+    for i in near_groups:
         take_raw(i)
+        take_ext(i)
         near(i)
 
     for d in range(1, groups):
@@ -248,6 +283,7 @@
     last = groups - 1
     far_part = total[last]
     take_raw(last)
+    take_ext(last)
     near(last)
     total[last] = total[last] + far_part
     send_y(last)
@@ -260,13 +296,12 @@
 
     for copy in sends:
         copy.wait_send()
-    ext_copy.wait_send()
 
     def end_piece(d, carry):
         piece_copy(d).wait_send()
         return carry
 
-    lax.fori_loop(1, n, end_piece, 0)
+    lax.fori_loop(1, half, end_piece, 0)
 
 
 def solution(mesh):
@@ -289,16 +324,17 @@
             out_specs=vmem,
             scratch_shapes=[
                 pltpu.VMEM((groups, slots, comps, tile, width), BF16),
-                pltpu.VMEM((pad, comps * columns), BF16),
-                pltpu.VMEM((quarter, comps * columns), BF16),
+                pltpu.VMEM((groups, pad, comps * width), BF16),
+                pltpu.VMEM((2, quarter, comps * width), BF16),
                 pltpu.VMEM((5, 1, tile), jnp.int32),
                 pltpu.VMEM((near_count, rows, rows), BF16),
                 pltpu.VMEM((far_count * rank, rows), BF16),
                 pltpu.VMEM((far_count * rank, coarse * rank), BF16),
                 pltpu.VMEM((near_count, tile, slots * tile + pad), BF16),
                 pltpu.VMEM((tile, slots * tile), BF16),
+                pltpu.VMEM((2, levels * rank, width), F32),
                 pltpu.VMEM((levels * rank, width), F32),
-                pltpu.VMEM((n, levels * rank, width), F32),
+                pltpu.VMEM((n // 2, levels * rank, width), F32),
                 pltpu.VMEM((coarse * rank, width), F32),
                 pltpu.VMEM((groups, coarse * rank, width), F32),
                 pltpu.VMEM((far_count * rank, columns), BF16),
@@ -308,8 +344,8 @@
                 dma((groups + 2,)),
                 dma((4,)), dma((5,)),
                 dma((groups, 5)), dma((groups, slots)),
-                dma((1,)), dma((1,)),
-                dma((n,)), dma((n,)),
+                dma((groups,)), dma((groups,)),
+                dma((n // 2,)), dma((n // 2 + 1,)),
                 dma((groups,)), dma((groups,)),
                 dma((groups,)), dma((groups,)),
             ],
@@ -319,7 +355,7 @@
         )(
             forces,
             order.reshape(1, tile),
-            bases.reshape(levels * rank, rows),
+            jnp.transpose(bases, (0, 2, 1, 3)),
             near_tiles.reshape(near_count, rows, rows),
             near_col,
             far_basis.reshape(far_count * rank, rows),

time: 71.3 us -> 51.8 us (0.73); the launches traced: 71.1 us -> 50.8 us
  Pallas kernels: 67.7 us -> 49 us
  local copies, waits for them, and re-layouts: 3.4 us -> 1.77 us
    pallas_call x1, Pallas kernels: 67.7 us -> 49 us  [on_device(): pl.pallas_call(functools.partial(kernel, n, groups, levels, rank), out_sh...]
    unnamed x3 -> x1, local copies, waits for them, and re-layouts: 3.4 us -> 1.77 us
where the time goes in v2:
time: 51.8 us; the launch traced here: 50.8 us
  Pallas kernels  49 us (95%)
  local copies, waits for them, and re-layouts  1.77 us (3%)
    pallas_call x1, Pallas kernels, on_device(): pl.pallas_call(functools.partial(kernel, n, groups, levels, rank), out_sh...  49 us
    unnamed x1, local copies, waits for them, and re-layouts  1.77 us

profile of v2, /device:TPU:9, one launch (start us, length us, event | category | flops | bytes accessed | tf_op | source)
XLA Modules:
  0.0 50.8 jit_solution(14147478873065347541)
XLA Ops:
  0.0 49.0 %shard_map.100 = f32[3,256,128]{2,1,0:T(8,128)} custom-call(bf16[3,256,512]{2,1,0:T(8,128)(2,1)} %forces.1, s32[1,256]{1,0:T(1,128)} %bitcast.9, bf16[2,3,32,256]{3,2,1,0:T(8,128)(2,1)} %bitcast.8, bf16[2,768,768]{2,1,0:T(8,128)(2,1)} %bitcast.5, s32[1,2]{1,0:T(1,128)} %near_col.1, bf16[512,768]{1,0:T(8,128)(2,1)} %bitcast.6, bf16[512,32]{1,0:T(8,128)(2,1)} %bitcast.7, ...), custom_call_target="tpu_custom_call" | custom-call | tf_op jit(solution)/shard_map/pallas_call | solution.py:320
  49.0 1.8 %copy.12 = f32[3,256,128]{2,1,0:T(8,128)} copy(f32[3,256,128]{2,1,0:T(8,128)} %shard_map.100) | data formatting | bytes 786432
